TPU v7x, 32 devices: a whole 2x2x4 slice. The times are simulated.
32 devices in a mesh: seq: 4 (over y, x), batch: 8 (over z, core).
Axes of the slice: x: 2, y: 2, z: 4, core: 2. Of those that a mesh axis runs over, the one named last changes fastest.
Arguments:
- activations: bfloat16 [8, 3072, 4096], P('batch', 'seq'), may hold values from -18 to 18
- out_grads: bfloat16 [8, 3072, 4096], P('batch', 'seq'), may hold values from -0.29882812 to 0.29882812
- lengths: int32 [8, 3], P('batch'), may hold values from 1 to 1536, 3072 in all within a row
Outputs:
- act_factor: float32 [4096, 4096], P(('seq', 'batch'))
- grad_factor: float32 [4096, 4096], P(('seq', 'batch'))
Inputs may be any that keep to these rules, and one draw needn't show every extreme that they name: `lengths`: each row sums to 3072 and its largest entry is exactly 1536.
All inputs are finite; a program needn't handle non-finite values.
Results may differ from a plain program's by a relative error of at most 0.004.
Values may be sent and summed in bfloat16 or wider, within the bound.
A program may use at most 64 MiB of HBM per device.

v0:
```python
import jax
import jax.numpy as jnp
from jax import lax
from jax.sharding import PartitionSpec as P


def local(activations, out_grads, lengths):
    act_local = activations[0]
    grad_local = out_grads[0]
    seq_lengths = lengths[0]
    tok_count = act_local.shape[0]
    width = act_local.shape[1]
    seq_count = seq_lengths.shape[0]
    group_size = lax.axis_size("seq")
    devices = group_size * lax.axis_size("batch")
    tile_rows = width // devices
    tile_start = lax.axis_index(("seq", "batch")) * tile_rows
    total_seqs = seq_count * lax.axis_size("batch")
    ends = jnp.cumsum(seq_lengths)
    starts = ends - seq_lengths
    position = lax.axis_index("seq") * tok_count + jnp.arange(tok_count, dtype=jnp.int32)
    member = (position[None, :] >= starts[:, None]) & (position[None, :] < ends[:, None])
    member = member.astype(jnp.bfloat16)
    act_part = jnp.dot(member, act_local, preferred_element_type=jnp.float32)
    grad_part = jnp.dot(member, grad_local, preferred_element_type=jnp.float32)
    act_sum, grad_sum = lax.psum((act_part, grad_part), "seq")
    act_rows = (act_sum / seq_lengths[:, None].astype(jnp.float32)).astype(jnp.bfloat16)
    grad_rows = grad_sum.astype(jnp.bfloat16)
    act_piece = lax.all_gather(act_rows, "batch", axis=0, tiled=True)
    grad_piece = lax.all_gather(grad_rows, "batch", axis=0, tiled=True)
    act_cols = lax.dynamic_slice_in_dim(act_piece, tile_start, tile_rows, 1)
    grad_cols = lax.dynamic_slice_in_dim(grad_piece, tile_start, tile_rows, 1)
    dims = (((0,), (0,)), ((), ()))
    act_new = lax.dot_general(act_cols, act_piece, dims, preferred_element_type=jnp.float32)
    grad_new = lax.dot_general(grad_cols, grad_piece, dims, preferred_element_type=jnp.float32)
    return (act_new / total_seqs, grad_new / total_seqs)


def solution(mesh):
    in_specs = (P("batch", "seq", None), P("batch", "seq", None), P("batch", None))
    out_specs = (P(("seq", "batch"), None), P(("seq", "batch"), None))
    return jax.shard_map(local, mesh=mesh, in_specs=in_specs, out_specs=out_specs, check_vma=False)
```

profile of v0, /device:TPU:0, one launch (start us, length us, event | category | flops | bytes accessed | tf_op | source)
XLA Modules:
  0.0 60.4 jit_solution(18398643600127713620)
XLA Ops:
  0.6 0.8 %reduce-window.7 = s32[3,1]{0,1:T(1,128)S(1)} reduce-window(s32[3,1]{0,1:T(1,128)} %bitcast.22, s32[]{:T(128)} %constant.7.clone.1), window={size=3x1 pad=2_0x0_0}, to_apply=%region_0.0 | reduce-window | flops 6 | bytes 28 | tf_op jit(solution)/shard_map/reduce-window.2
  1.5 0.0 copy-start
  1.5 0.8 %bitcast_subtract_fusion = s32[3]{0:T(128)S(1)} fusion(s32[1,3]{1,0:T(1,128)} %param.5, s32[3,1]{0,1:T(1,128)S(1)} %reduce-window.7), kind=kLoop, calls=%fused_computation.14 | loop fusion | flops 3 | bytes 36 | tf_op jit(solution)/shard_map/sub | solution.py:20
  2.3 0.8 %bitcast_convert_fusion = f32[3]{0:T(128)S(1)} fusion(s32[1,3]{1,0:T(1,128)} %param.5), kind=kLoop, calls=%fused_computation.13 | loop fusion | flops 3 | bytes 24 | tf_op jit(solution)/shard_map/convert_element_type | solution.py:27
  3.1 4.0 %fusion = f32[3,4096]{1,0:T(4,128)S(1)} fusion(bf16[1,768,4096]{2,1,0:T(8,128)(2,1)} %param.4, s32[768]{0:T(1024)S(1)} %iota_add_fusion, s32[3]{0:T(128)S(1)} %bitcast.20, s32[3]{0:T(128)S(1)} %bitcast_subtract_fusion), kind=kOutput, calls=%fused_computation | convolution fusion | flops 18881280 | bytes 6343704 | tf_op jit(solution)/shard_map/dot_general | solution.py:25
  7.1 0.0 copy-done
  7.1 1.0 %fusion.2 = f32[3,4096]{1,0:T(4,128)S(1)} fusion(bf16[1,768,4096]{2,1,0:T(8,128)(2,1)S(1)} %copy-done, s32[768]{0:T(1024)S(1)} %iota_add_fusion, s32[3]{0:T(128)S(1)} %bitcast.21, s32[3]{0:T(128)S(1)} %bitcast_subtract_fusion), kind=kOutput, calls=%fused_computation.2 | convolution fusion | flops 18881280 | bytes 6343704 | tf_op jit(solution)/shard_map/dot_general | solution.py:24
  8.0 19.8 %all-reduce.2 = (f32[3,4096]{1,0:T(4,128)S(1)}, bf16[3,4096]{1,0:T(4,128)(2,1)S(1)}) all-reduce(f32[3,4096]{1,0:T(4,128)S(1)} %fusion.2, f32[3,4096]{1,0:T(4,128)S(1)} %fusion), channel_id=1, replica_groups=mesh['seq'=4,'batch'=8] {'seq'}, use_global_device_ids=true, to_apply=%region_1.2 | all-reduce | flops 24576 | bytes 172032 | tf_op jit(solution)/shard_map/psum | solution.py:26
  27.8 0.1 fusion.4
  27.9 14.4 %all-gather.1 = bf16[8,3,4096]{2,1,0:T(4,128)(2,1)S(1)} all-gather(bf16[1,3,4096]{2,1,0:T(4,128)(2,1)S(1)} %bitcast.19), channel_id=1, replica_groups=mesh['seq'=4,'batch'=8] {'batch'}, dimensions={0}, use_global_device_ids=true | all-gather | bytes 221184 | tf_op jit(solution)/shard_map/all_gather | solution.py:30
  42.3 0.2 reshape.48
  42.5 14.2 %all-gather = bf16[8,3,4096]{2,1,0:T(4,128)(2,1)S(1)} all-gather(bf16[1,3,4096]{2,1,0:T(4,128)(2,1)S(1)} %fusion.4), channel_id=1, replica_groups=mesh['seq'=4,'batch'=8] {'batch'}, dimensions={0}, use_global_device_ids=true | all-gather | bytes 221184 | tf_op jit(solution)/shard_map/all_gather | solution.py:29
  56.7 0.2 reshape.46
  56.9 1.8 %convolution_multiply_fusion.1 = f32[128,4096]{1,0:T(8,128)} fusion(bf16[24,4096]{1,0:T(8,128)(2,1)S(1)} %reshape.46, s32[]{:T(128)S(6)} %select_n.4), kind=kOutput, calls=%fused_computation.5 | convolution fusion | flops 25690112 | bytes 2299908 | tf_op jit(solution)/shard_map/dot_general | solution.py:34
  58.7 1.8 %convolution_multiply_fusion = f32[128,4096]{1,0:T(8,128)} fusion(bf16[24,4096]{1,0:T(8,128)(2,1)S(1)} %reshape.48, s32[]{:T(128)S(6)} %select_n.4), kind=kOutput, calls=%fused_computation.4 | convolution fusion | flops 25690112 | bytes 2299908 | tf_op jit(solution)/shard_map/dot_general | solution.py:35
  (1 shorter events, 0.0 us)
Async XLA Ops:
  1.5 5.6 %copy-start = (bf16[1,768,4096]{2,1,0:T(8,128)(2,1)S(1)}, bf16[1,768,4096]{2,1,0:T(8,128)(2,1)}, u32[]{:S(2)}) copy-start(bf16[1,768,4096]{2,1,0:T(8,128)(2,1)} %param.3) | copy-start | bytes 18874372
where the time goes:
time: 60.7 us; the launch traced here: 60.4 us
  blocking collectives  48.4 us (80%)
  matrix products  8.53 us (14%)
  other arithmetic  2.51 us (4%)
  between operations  0.67 us (1%)
    psum x1, blocking collectives, local(): act_sum, grad_sum = lax.psum((act_part, grad_part), 'seq')  19.8 us
    all_gather x1, blocking collectives, local(): grad_piece = lax.all_gather(grad_rows, 'batch', axis=0, tiled=True)  14.4 us
    all_gather x1, blocking collectives, local(): act_piece = lax.all_gather(act_rows, 'batch', axis=0, tiled=True)  14.2 us
    dot_general x1, matrix products, local(): grad_part = jnp.dot(member, grad_local, preferred_element_type=jnp.float32)  3.99 us
    dot_general x1, matrix products, local(): lax.dot_general(act_cols, act_piece, dims, preferred_element_type=jnp.flo...  1.79 us
    dot_general x1, matrix products, local(): lax.dot_general(grad_cols, grad_piece, dims, preferred_element_type=jnp.f...  1.78 us

commit v1 on v0

--- a/solution.py
+++ b/solution.py
@@ -5,6 +5,12 @@
 
 
 def local(activations, out_grads, lengths):
+
+    def spread_the_unit(array_in, incoming_x):
+        v_now = jnp.concatenate([array_in, incoming_x], 1)
+        local_now = jax.lax.all_gather(v_now, "batch", axis=0, tiled=True)
+        return jnp.split(local_now, [array_in.shape[1]], 1)
+
     act_local = activations[0]
     grad_local = out_grads[0]
     seq_lengths = lengths[0]
@@ -26,8 +32,7 @@
     act_sum, grad_sum = lax.psum((act_part, grad_part), "seq")
     act_rows = (act_sum / seq_lengths[:, None].astype(jnp.float32)).astype(jnp.bfloat16)
     grad_rows = grad_sum.astype(jnp.bfloat16)
-    act_piece = lax.all_gather(act_rows, "batch", axis=0, tiled=True)
-    grad_piece = lax.all_gather(grad_rows, "batch", axis=0, tiled=True)
+    act_piece, grad_piece = spread_the_unit(act_rows, incoming_x=grad_rows)
     act_cols = lax.dynamic_slice_in_dim(act_piece, tile_start, tile_rows, 1)
     grad_cols = lax.dynamic_slice_in_dim(grad_piece, tile_start, tile_rows, 1)
     dims = (((0,), (0,)), ((), ()))

time: 60.7 us -> 47.3 us (0.78)
  blocking collectives: 48.4 us -> 35 us
    all_gather x2 -> x1, blocking collectives: 28.6 us -> 15.2 us  [spread_the_unit(): local_now = jax.lax.all_gather(v_now, 'batch', axis=0, tiled=True)]
where the time goes in v1:
time: 47.3 us; the launch traced here: 47.1 us
  blocking collectives  35 us (74%)
  matrix products  8.53 us (18%)
  other arithmetic  2.54 us (5%)
  between operations  0.68 us (1%)
    psum x1, blocking collectives, local(): act_sum, grad_sum = lax.psum((act_part, grad_part), 'seq')  19.7 us
    all_gather x1, blocking collectives, spread_the_unit(): local_now = jax.lax.all_gather(v_now, 'batch', axis=0, tiled=True)  15.2 us
    dot_general x1, matrix products, local(): grad_part = jnp.dot(member, grad_local, preferred_element_type=jnp.float32)  3.99 us
    dot_general x1, matrix products, local(): lax.dot_general(grad_cols, grad_piece, dims, preferred_element_type=jnp.f...  1.79 us
    dot_general x1, matrix products, local(): lax.dot_general(act_cols, act_piece, dims, preferred_element_type=jnp.flo...  1.78 us
    dot_general x1, matrix products, local(): act_part = jnp.dot(member, act_local, preferred_element_type=jnp.float32)  0.96 us

profile of v1, /device:TPU:0, one launch (start us, length us, event | category | flops | bytes accessed | tf_op | source)
XLA Modules:
  0.0 47.1 jit_solution(4271760519261514999)
XLA Ops:
  0.6 0.8 %reduce-window.7 = s32[3,1]{0,1:T(1,128)S(1)} reduce-window(s32[3,1]{0,1:T(1,128)} %bitcast.18, s32[]{:T(128)} %constant.7.clone.1), window={size=3x1 pad=2_0x0_0}, to_apply=%region_0.0 | reduce-window | flops 6 | bytes 28 | tf_op jit(solution)/shard_map/reduce-window.2
  1.5 0.0 copy-start
  1.5 0.8 %bitcast_subtract_fusion = s32[3]{0:T(128)S(1)} fusion(s32[1,3]{1,0:T(1,128)} %param.5, s32[3,1]{0,1:T(1,128)S(1)} %reduce-window.7), kind=kLoop, calls=%fused_computation.13 | loop fusion | flops 3 | bytes 36 | tf_op jit(solution)/shard_map/sub | solution.py:26
  2.3 0.8 %bitcast_convert_fusion = f32[3]{0:T(128)S(1)} fusion(s32[1,3]{1,0:T(1,128)} %param.5), kind=kLoop, calls=%fused_computation.12 | loop fusion | flops 3 | bytes 24 | tf_op jit(solution)/shard_map/convert_element_type | solution.py:33
  3.1 4.0 %fusion = f32[3,4096]{1,0:T(4,128)S(1)} fusion(bf16[1,768,4096]{2,1,0:T(8,128)(2,1)} %param.4, s32[768]{0:T(1024)S(1)} %iota_add_fusion, s32[3]{0:T(128)S(1)} %bitcast.16, s32[3]{0:T(128)S(1)} %bitcast_subtract_fusion), kind=kOutput, calls=%fused_computation | convolution fusion | flops 18881280 | bytes 6343704 | tf_op jit(solution)/shard_map/dot_general | solution.py:31
  7.1 0.0 copy-done
  7.1 1.0 %fusion.2 = f32[3,4096]{1,0:T(4,128)S(1)} fusion(bf16[1,768,4096]{2,1,0:T(8,128)(2,1)S(1)} %copy-done, s32[768]{0:T(1024)S(1)} %iota_add_fusion, s32[3]{0:T(128)S(1)} %bitcast.17, s32[3]{0:T(128)S(1)} %bitcast_subtract_fusion), kind=kOutput, calls=%fused_computation.2 | convolution fusion | flops 18881280 | bytes 6343704 | tf_op jit(solution)/shard_map/dot_general | solution.py:30
  8.0 19.7 %all-reduce.2 = (bf16[3,4096]{1,0:T(4,128)(2,1)S(1)}, f32[3,4096]{1,0:T(4,128)S(1)}) all-reduce(f32[3,4096]{1,0:T(4,128)S(1)} %fusion, f32[3,4096]{1,0:T(4,128)S(1)} %fusion.2), channel_id=1, replica_groups=mesh['seq'=4,'batch'=8] {'seq'}, use_global_device_ids=true, to_apply=%region_2.3 | all-reduce | flops 24576 | bytes 172032 | tf_op jit(solution)/shard_map/psum | solution.py:32
  27.8 0.1 divide_convert_fusion
  27.9 15.2 %all-gather = bf16[8,3,8192]{2,1,0:T(4,128)(2,1)S(1)} all-gather(bf16[1,3,8192]{2,1,0:T(4,128)(2,1)S(1)} %maximum_bitcast_fusion), channel_id=1, replica_groups=mesh['seq'=4,'batch'=8] {'batch'}, dimensions={0}, use_global_device_ids=true | all-gather | bytes 442368 | tf_op jit(solution)/shard_map/all_gather | solution.py:11
  43.1 0.3 reshape.46
  43.5 1.8 %convolution_multiply_fusion = f32[128,4096]{1,0:T(8,128)} fusion(bf16[24,4096]{1,0:T(8,128)(2,1)S(1)} %get-tuple-element.4, s32[]{:T(128)S(6)} %select_n.4), kind=kOutput, calls=%fused_computation.4 | convolution fusion | flops 25690112 | bytes 2299908 | tf_op jit(solution)/shard_map/dot_general | solution.py:40
  45.3 1.8 %convolution_multiply_fusion.1 = f32[128,4096]{1,0:T(8,128)} fusion(bf16[24,4096]{1,0:T(8,128)(2,1)S(1)} %get-tuple-element.5, s32[]{:T(128)S(6)} %select_n.4), kind=kOutput, calls=%fused_computation.5 | convolution fusion | flops 25690112 | bytes 2299908 | tf_op jit(solution)/shard_map/dot_general | solution.py:39
  (3 shorter events, 0.1 us)
Async XLA Ops:
  1.5 5.6 %copy-start = (bf16[1,768,4096]{2,1,0:T(8,128)(2,1)S(1)}, bf16[1,768,4096]{2,1,0:T(8,128)(2,1)}, u32[]{:S(2)}) copy-start(bf16[1,768,4096]{2,1,0:T(8,128)(2,1)} %param.3) | copy-start | bytes 18874372
